TPU v7x, 32 devices: a whole 2x2x4 slice. The times are simulated.
32 devices in a mesh: ga: 8 (over z, y), ba: 4 (over x, core).
Axes of the slice: x: 2, y: 2, z: 4, core: 2. Of those that a mesh axis runs over, the one named last changes fastest.
Arguments:
- coefficients: bfloat16 [10240, 6144], P('ga', 'ba')
- rotation: bfloat16 [6144, 6144], P('ga', 'ba'), may hold values from -0.078125 to 0.078125
Outputs:
- new_coefficients: bfloat16 [10240, 6144], P('ga', 'ba')
- band_rms: float32 [6144], P('ba')
All inputs are finite; a program needn't handle non-finite values.
Results may differ from a plain program's by a relative error of at most 0.0004.
Values may be sent and summed in bfloat16 or wider, within the bound.
A program may use at most 128 MiB of HBM per device.

v0:
```python
import jax
import jax.numpy as jnp
from jax import lax
from jax.sharding import PartitionSpec as P


def body(coefficients, rotation):
    all_bands = lax.all_gather(coefficients, "ba", axis=1, tiled=True)
    rotated = jnp.dot(
        all_bands,
        lax.all_gather(rotation, "ga", axis=0, tiled=True),
        preferred_element_type=jnp.float32,
    )
    squares = lax.psum(jnp.sum(rotated * rotated, axis=0), "ga")
    total_rows = coefficients.shape[0] * lax.axis_size("ga")
    band_rms = jnp.sqrt(squares / total_rows + 1e-06)
    return ((rotated / band_rms).astype(jnp.bfloat16), band_rms)


def solution(mesh):
    in_specs = (P("ga", "ba"), P("ga", "ba"))
    out_specs = (P("ga", "ba"), P("ba"))
    return jax.shard_map(body, mesh=mesh, in_specs=in_specs, out_specs=out_specs, check_vma=False)
```

profile of v0, /device:TPU:0, one launch (start us, length us, event | category | flops | bytes accessed | tf_op | source)
XLA Modules:
  0.0 543.6 jit_solution(14183646409815637874)
XLA Ops:
  7.2 0.0 all-gather.3.cloned.1.call-start
  7.2 0.7 all-gather.3.cloned.1.call-update
  7.9 0.0 all-gather.5.cloned.1.call-start
  7.9 0.7 all-gather.5.cloned.1.call-update
  8.6 103.6 %all-gather.3.cloned.1.call-done = bf16[1280,6144]{1,0:T(8,128)(2,1)} async-done(((bf16[1280,1536]{1,0:T(8,128)(2,1)}), bf16[1280,6144]{1,0:T(8,128)(2,1)}) %all-gather.3.cloned.1.call-update) | async-done | bytes 15728656 | tf_op jit(solution)/shard_map/all_gather | solution.py:8
  112.2 364.0 %all-gather.5.cloned.1.call-done = bf16[6144,1536]{1,0:T(8,128)(2,1)} async-done(((bf16[768,1536]{1,0:T(8,128)(2,1)}), bf16[6144,1536]{1,0:T(8,128)(2,1)}) %all-gather.5.cloned.1.call-update) | async-done | bytes 18874384 | tf_op jit(solution)/shard_map/all_gather | solution.py:11
  476.2 33.9 %multiply_reduce_fusion = (f32[1536]{0:T(1024)S(1)}, f32[1280,1536]{1,0:T(8,128)}) fusion(bf16[1280,6144]{1,0:T(8,128)(2,1)} %all-gather.3.cloned.1.call-done, bf16[6144,1536]{1,0:T(8,128)(2,1)} %all-gather.5.cloned.1.call-done), kind=kOutput, calls=%fused_computation.1 | convolution fusion | flops 24163121152 | bytes 42473472 | tf_op jit(solution)/shard_map/dot_general | solution.py:9
  510.1 20.4 %psum.7 = f32[1536]{0:T(1024)S(1)} all-reduce(f32[1536]{0:T(1024)S(1)} %get-tuple-element.2), channel_id=1, replica_groups=mesh['ga'=8,'ba'=4] {'ga'}, use_global_device_ids=true, to_apply=%region_1.0 | all-reduce | flops 1536 | bytes 12288 | tf_op jit(solution)/shard_map/psum | solution.py:14
  530.6 0.0 copy-start
  530.6 6.2 %divide_convert_fusion = bf16[1280,1536]{1,0:T(8,128)(2,1)} fusion(f32[1280,1536]{1,0:T(8,128)} %get-tuple-element.3, f32[1536]{0:T(1024)S(1)} %add_sqrt_fusion), kind=kLoop, calls=%fused_computation | loop fusion | flops 3932160 | bytes 11802624 | tf_op jit(solution)/shard_map/convert_element_type | solution.py:17
  536.8 0.0 copy-done
  (1 shorter events, 0.0 us)
Async XLA Ops:
  7.2 105.1 %all-gather.3.cloned.1.call-start = ((), (), s32[]{:S(2)}) async-start(), calls=%async_computation | async-start | bytes 19660800 | tf_op jit(solution)/shard_map/all_gather | solution.py:8
  7.9 468.3 %all-gather.5.cloned.1.call-start = ((), (), s32[]{:S(2)}) async-start(), calls=%async_computation.1 | async-start | bytes 21233664 | tf_op jit(solution)/shard_map/all_gather | solution.py:11
  530.6 6.2 %copy-start = (f32[1536]{0:T(1024)}, f32[1536]{0:T(1024)S(1)}, u32[]{:S(2)}) copy-start(f32[1536]{0:T(1024)S(1)} %add_sqrt_fusion) | copy-start | bytes 18436
Sparse Core Ops, SparseCore 0:
  9.5 102.6 all-gather.2
  113.8 362.3 all-gather.4
where the time goes:
time: 544 us
  waiting for transfers between devices  469 us (86%)
  matrix products  33.9 us (6%)
  blocking collectives  20.4 us (4%)
  between operations  14.1 us (3%)
  other arithmetic  6.19 us (1%)
    all_gather x1, waiting for transfers between devices, body(): lax.all_gather(rotation, 'ga', axis=0, tiled=True)  364 us
    all_gather x1, waiting for transfers between devices, body(): all_bands = lax.all_gather(coefficients, 'ba', axis=1, tiled=True)  104 us
    dot_general x1, matrix products, body(): jnp.dot(all_bands, lax.all_gather(rotation, 'ga', axis=0, tiled=True), pr...  33.9 us
    psum x1, blocking collectives, body(): squares = lax.psum(jnp.sum(rotated * rotated, axis=0), 'ga')  20.4 us
  transfers between devices with their start and end apart: 2, of which 2 were waited for; matrix products, arithmetic and copies ran while one was open for 0% of the time, Pallas kernels for 0%

commit v1 on v0

v1 whole, which is shorter than its diff:
```python
import functools
import math

import jax
import jax.numpy as jnp
from jax import lax
from jax.experimental import pallas as pl
from jax.experimental.pallas import tpu as pltpu
from jax.sharding import PartitionSpec as P

MESH = pl.DeviceIdType.MESH
CHUNKS = 6


def kernel(n_ga, n_ba, line, coef, rot, out, rms_out, a_buf, b_buf, total, stats,
           recv, send_z, send_zb, send_y, a_recv, a_send_x, a_send_p, s_recv, s_send, own):
    lanes = n_ga // line
    depth = rot.shape[0]
    rows, width = coef.shape
    piece = depth // CHUNKS
    span = lanes * depth
    me, mb = lax.axis_index("ga"), lax.axis_index("ba")
    z, w = me // lanes, lax.rem(me, lanes)
    bx, bc = mb // 2, lax.rem(mb, 2)
    half = n_ba // 2

    def ga(i):
        return {"ga": i}

    def side(o):
        return lax.rem(w + o, lanes)

    def chunk(index):
        return b_buf.at[pl.ds(pl.multiple_of(index * piece, piece), piece)]

    barrier = pltpu.get_barrier_semaphore()
    for o in range(1, n_ga):
        pl.semaphore_signal(barrier, inc=1, device_id=ga(lax.rem(me + o, n_ga)), device_id_type=MESH)
    for o in range(1, n_ba):
        pl.semaphore_signal(barrier, inc=1, device_id={"ba": lax.rem(mb + o, n_ba)}, device_id_type=MESH)

    mine = [
        pltpu.make_async_copy(rot, b_buf.at[pl.ds(pl.multiple_of(me * depth, depth), depth)], own.at[0]),
        pltpu.make_async_copy(coef, a_buf.at[mb], own.at[1]),
    ]
    for copy in mine:
        copy.start()
    pl.semaphore_wait(barrier, n_ga - 1 + n_ba - 1)

    def remote(src, index, sem, target):
        return pltpu.make_async_remote_copy(
            src_ref=src, dst_ref=chunk(index), send_sem=sem, recv_sem=recv.at[index],
            device_id=ga(target), device_id_type=MESH)

    def arrived(index):
        pltpu.make_async_copy(chunk(index), chunk(index), recv.at[index]).wait()

    def along(k, src, index, sem):
        @pl.when(z < line - 1 if k == 0 else z > 0)
        def _():
            remote(src, index, sem, me + lanes if k == 0 else me - lanes).start()

    def across(src, index, from_z):
        for o in range(1, lanes):
            remote(src, index, send_y.at[o - 1, from_z], z * lanes + side(o)).start()

    def own_chunk(q):
        return rot.at[pl.ds(q * piece, piece)]

    last = CHUNKS - 1
    across(own_chunk(last), me * CHUNKS + last, z)
    for q in range(CHUNKS):
        for k in range(2):
            along(k, own_chunk(q), me * CHUNKS + q, send_z.at[k, z])
        if q < last:
            across(own_chunk(q), me * CHUNKS + q, z)

    def a_copy(src, index, sem, target):
        return pltpu.make_async_remote_copy(
            src_ref=src, dst_ref=a_buf.at[index], send_sem=sem, recv_sem=a_recv.at[index],
            device_id={"ba": target}, device_id_type=MESH)

    partner = mb + 1 - 2 * bc
    far = [lax.rem(bx + o, half) * 2 + bc for o in range(1, half)]
    for o, target in enumerate(far):
        a_copy(coef, mb, a_send_x.at[o], target).start()
    a_copy(coef, mb, a_send_p.at[mb], partner).start()

    for o in range(1, lanes):
        index = (z * lanes + side(o)) * CHUNKS + last
        arrived(index)
        for k in range(2):
            along(k, chunk(index), index, send_zb.at[k, z * lanes + side(o)])

    tile = math.gcd(rows, 256)

    def multiply(j, dist):
        from_z = z - dist + 2 * dist * j

        @pl.when((from_z >= 0) & (from_z < line) & ((dist > 0) | (j == 0)))
        def _():
            for o in range(1, lanes):
                for q in range(last):
                    arrived((from_z * lanes + side(o)) * CHUNKS + q)
            begin = from_z * span
            at, column = begin // width, pl.multiple_of(lax.rem(begin, width), 128)

            @pl.loop(0, rows // tile)
            def _(t):
                part = pl.ds(pl.multiple_of(t * tile, tile), tile)
                product = jnp.dot(
                    a_buf[at, part, pl.ds(column, span)],
                    b_buf[pl.ds(pl.multiple_of(begin, span), span), :],
                    preferred_element_type=jnp.float32)

                @pl.when(dist == 0)
                def _():
                    total[part, :] = product

                @pl.when(dist > 0)
                def _():
                    total[part, :] += product

    def at_distance(dist):
        lax.fori_loop(0, 2, lambda j, c: (multiply(j, dist), c)[1], 0)

    def relay(d, carry):
        for q in range(CHUNKS + lanes - 1):
            for k in range(2):
                from_z = z - d if k == 0 else z + d

                @pl.when((from_z >= 0) & (from_z < line))
                def _():
                    lane = w if q < CHUNKS else side(q - CHUNKS + 1)
                    block = from_z * lanes + lane
                    index = block * CHUNKS + min(q, last)
                    arrived(index)
                    along(k, chunk(index), index, send_z.at[k, from_z] if q < CHUNKS else send_zb.at[k, block])
                    if q < last:
                        across(chunk(index), index, from_z)

            if q == 2:
                @pl.when(d == 2)
                def _():
                    for source in far:
                        pltpu.make_async_copy(a_buf.at[source], a_buf.at[source], a_recv.at[source]).wait()
                        a_copy(a_buf.at[source], source, a_send_p.at[source], partner).start()

            if q == 1:
                @pl.when(d == line - 1)
                def _():
                    at_distance(line - 3)

            if q == last:
                @pl.when(d == 2)
                def _():
                    for copy in mine:
                        copy.wait()
                    for x in range(half):
                        source = x * 2 + 1 - bc
                        pltpu.make_async_copy(a_buf.at[source], a_buf.at[source], a_recv.at[source]).wait()

                @pl.when(d >= 2)
                def _():
                    at_distance(d - 2 + d // (line - 1))
        return carry

    lax.fori_loop(1, line, relay, 0)
    at_distance(line - 1)

    def squares(t, c):
        v = total[pl.ds(pl.multiple_of(t * tile, tile), tile), :]
        return c + jnp.sum(v * v, axis=0, keepdims=True)

    stats[me] = lax.fori_loop(0, rows // tile, squares, jnp.zeros((1, total.shape[1]), jnp.float32))

    def share(o, target, slot):
        return pltpu.make_async_remote_copy(
            src_ref=stats.at[me], dst_ref=stats.at[me], send_sem=s_send.at[o], recv_sem=s_recv.at[slot],
            device_id=ga(target), device_id_type=MESH)

    for o in range(1, n_ga):
        share(o, lax.rem(me + o, n_ga), me).start()
    for o in range(1, n_ga):
        source = lax.rem(me + o, n_ga)
        pltpu.make_async_copy(stats.at[source], stats.at[source], s_recv.at[source]).wait()
    everything = stats[0]
    for g in range(1, n_ga):
        everything = everything + stats[g]
    rms = jnp.sqrt(everything / (rows * n_ga) + 1e-06)
    rms_out[...] = rms
    scale = 1.0 / rms

    @pl.loop(0, rows // tile)
    def _(t):
        part = pl.ds(pl.multiple_of(t * tile, tile), tile)
        out[part, :] = (total[part, :] * scale).astype(jnp.bfloat16)

    for o in range(1, n_ga):
        share(o, lax.rem(me + o, n_ga), me).wait_send()
    for o, target in enumerate(far):
        a_copy(coef, mb, a_send_x.at[o], target).wait_send()
    for x in range(half):
        a_copy(coef, x * 2 + bc, a_send_p.at[x * 2 + bc], partner).wait_send()

    def sent(count, sem):
        view = b_buf.at[pl.ds(0, count * piece)]
        pltpu.make_async_copy(view, view, sem).wait()

    for from_z in range(line):
        for k in range(2):
            @pl.when((z >= from_z) & (z < line - 1) if k == 0 else (z <= from_z) & (z > 0))
            def _():
                sent(CHUNKS, send_z.at[k, from_z])
                for o in range(1, lanes):
                    sent(1, send_zb.at[k, from_z * lanes + side(o)])
        for o in range(1, lanes):
            @pl.when(z == from_z)
            def _():
                sent(CHUNKS, send_y.at[o - 1, from_z])

            @pl.when(z != from_z)
            def _():
                sent(last, send_y.at[o - 1, from_z])


def solution(mesh):
    n_ga, n_ba = mesh.shape["ga"], mesh.shape["ba"]
    line = 2 ** math.ceil(math.log2(n_ga) / 2)
    lanes = n_ga // line

    def body(coef, rot):
        rows, width = coef.shape
        depth, columns = rot.shape
        dma = pltpu.SemaphoreType.DMA
        out, rms = pl.pallas_call(
            functools.partial(kernel, n_ga, n_ba, line),
            out_shape=(jax.ShapeDtypeStruct((rows, columns), jnp.bfloat16),
                       jax.ShapeDtypeStruct((1, columns), jnp.float32)),
            in_specs=[pl.BlockSpec(memory_space=pl.ANY)] * 2,
            out_specs=(pl.BlockSpec(memory_space=pltpu.VMEM),) * 2,
            scratch_shapes=[
                pltpu.VMEM((n_ba, rows, width), jnp.bfloat16),
                pltpu.VMEM((n_ga * depth, columns), jnp.bfloat16),
                pltpu.VMEM((rows, columns), jnp.float32),
                pltpu.VMEM((n_ga, 1, columns), jnp.float32),
                dma((n_ga * CHUNKS,)),
                dma((2, line)),
                dma((2, n_ga)),
                dma((lanes - 1, line)),
                dma((n_ba,)),
                dma((n_ba // 2 - 1,)),
                dma((n_ba,)),
                dma((n_ga,)),
                dma((n_ga,)),
                dma((2,)),
            ],
            compiler_params=pltpu.CompilerParams(
                collective_id=0, has_side_effects=True, vmem_limit_bytes=67043328),
        )(coef, rot)
        return out, rms.reshape(columns)

    return jax.shard_map(body, mesh=mesh, in_specs=(P("ga", "ba"), P("ga", "ba")),
                         out_specs=(P("ga", "ba"), P("ba")), check_vma=False)
```

time: 544 us -> 206 us (0.38)
  waiting for transfers between devices: 469 us -> 0 us
  Pallas kernels: 0 us -> 199 us
  matrix products: 33.9 us -> 0 us
  blocking collectives: 20.4 us -> 0 us
  between operations: 14.1 us -> 0.64 us
    all_gather x2 -> x0, waiting for transfers between devices: 468 us -> none  [the longest x1 364 us: body(): lax.all_gather(rotation, 'ga', axis=0, tiled=True)]
    pallas_call x0 -> x1, Pallas kernels: none -> 199 us  [body(): pl.pallas_call(functools.partial(kernel, n_ga, n_ba, line), out_shape=(ja...]
    dot_general x1 -> x0, matrix products: 33.9 us -> none  [body(): jnp.dot(all_bands, lax.all_gather(rotation, 'ga', axis=0, tiled=True), pr...]
    psum x1 -> x0, blocking collectives: 20.4 us -> none  [body(): squares = lax.psum(jnp.sum(rotated * rotated, axis=0), 'ga')]
    convert_element_type x1 -> x0, other arithmetic: 6.18 us -> none  [body(): return ((rotated / band_rms).astype(jnp.bfloat16), band_rms)]
  transfers between devices with their start and end apart: 2 -> 0, of which waited for: 2 -> 0; matrix products, arithmetic and copies ran while one was open for 0% -> 0% of each run, Pallas kernels for 0% -> 0%
where the time goes in v1:
time: 206 us; the launch traced here: 205 us
  Pallas kernels  199 us (97%)
  local copies, waits for them, and re-layouts  4.29 us (2%)
    pallas_call x1, Pallas kernels, body(): pl.pallas_call(functools.partial(kernel, n_ga, n_ba, line), out_shape=(ja...  199 us
    unnamed x1, local copies, waits for them, and re-layouts  4.29 us

profile of v1, /device:TPU:0, one launch (start us, length us, event | category | flops | bytes accessed | tf_op | source)
XLA Modules:
  0.0 205.4 jit_solution(571086395772664087)
XLA Ops:
  0.6 199.1 %shard_map.41 = (bf16[1280,1536]{1,0:T(8,128)(2,1)}, f32[1,1536]{1,0:T(1,128)}) custom-call(bf16[1280,1536]{1,0:T(8,128)(2,1)} %coef.1, bf16[768,1536]{1,0:T(8,128)(2,1)} %rot.1), custom_call_target="tpu_custom_call" | custom-call | tf_op jit(solution)/shard_map/pallas_call | solution.py:236
  199.8 1.3 reduce
  201.1 4.3 %copy.5 = bf16[1280,1536]{1,0:T(8,128)(2,1)} copy(bf16[1280,1536]{1,0:T(8,128)(2,1)} %get-tuple-element.8) | data formatting | bytes 7864320

commit v2 on v1

--- a/solution.py
+++ b/solution.py
@@ -10,9 +10,10 @@
 
 MESH = pl.DeviceIdType.MESH
 CHUNKS = 6
-
-
-def kernel(n_ga, n_ba, line, coef, rot, out, rms_out, a_buf, b_buf, total, stats,
+CROSS = 1
+
+
+def kernel(n_ga, n_ba, line, coef, rot, total, rms_out, a_buf, b_buf, stats,
            recv, send_z, send_zb, send_y, a_recv, a_send_x, a_send_p, s_recv, s_send, own):
     lanes = n_ga // line
     depth = rot.shape[0]
@@ -67,8 +68,10 @@
     def own_chunk(q):
         return rot.at[pl.ds(q * piece, piece)]
 
-    last = CHUNKS - 1
-    across(own_chunk(last), me * CHUNKS + last, z)
+    last = CHUNKS - CROSS
+    crossed = [(o, q) for q in range(last, CHUNKS) for o in range(1, lanes)]
+    for q in range(last, CHUNKS):
+        across(own_chunk(q), me * CHUNKS + q, z)
     for q in range(CHUNKS):
         for k in range(2):
             along(k, own_chunk(q), me * CHUNKS + q, send_z.at[k, z])
@@ -86,72 +89,99 @@
         a_copy(coef, mb, a_send_x.at[o], target).start()
     a_copy(coef, mb, a_send_p.at[mb], partner).start()
 
-    for o in range(1, lanes):
-        index = (z * lanes + side(o)) * CHUNKS + last
+    for o, q in crossed:
+        index = (z * lanes + side(o)) * CHUNKS + q
         arrived(index)
         for k in range(2):
             along(k, chunk(index), index, send_zb.at[k, z * lanes + side(o)])
 
     tile = math.gcd(rows, 256)
 
-    def multiply(j, dist):
+    def multiply(j, dist, part):
         from_z = z - dist + 2 * dist * j
 
         @pl.when((from_z >= 0) & (from_z < line) & ((dist > 0) | (j == 0)))
         def _():
+            if part == "all":
+                for o in range(1, lanes):
+                    for q in range(last):
+                        arrived((from_z * lanes + side(o)) * CHUNKS + q)
+                panel(from_z * span, span, dist)
+                return
+            if part == "own":
+                panel((from_z * lanes + w) * depth, depth, dist)
+                return
             for o in range(1, lanes):
-                for q in range(last):
-                    arrived((from_z * lanes + side(o)) * CHUNKS + q)
-            begin = from_z * span
-            at, column = begin // width, pl.multiple_of(lax.rem(begin, width), 128)
-
-            @pl.loop(0, rows // tile)
-            def _(t):
-                part = pl.ds(pl.multiple_of(t * tile, tile), tile)
-                product = jnp.dot(
-                    a_buf[at, part, pl.ds(column, span)],
-                    b_buf[pl.ds(pl.multiple_of(begin, span), span), :],
-                    preferred_element_type=jnp.float32)
-
-                @pl.when(dist == 0)
-                def _():
-                    total[part, :] = product
-
-                @pl.when(dist > 0)
-                def _():
-                    total[part, :] += product
-
-    def at_distance(dist):
-        lax.fori_loop(0, 2, lambda j, c: (multiply(j, dist), c)[1], 0)
+                block = from_z * lanes + side(o)
+                for q in range(cut):
+                    arrived(block * CHUNKS + q)
+                panel(block * depth, cut * piece, dist)
+                for q in range(cut, last):
+                    arrived(block * CHUNKS + q)
+                panel(block * depth + cut * piece, depth - cut * piece, dist)
+
+    cut = max(q for q in range(last) if q * piece % 128 == 0) if depth % 128 == 0 else 0
+
+    def panel(begin, size, dist):
+        at, column = begin // width, pl.multiple_of(lax.rem(begin, width), 128)
+
+        @pl.loop(0, rows // tile)
+        def _(t):
+            part = pl.ds(pl.multiple_of(t * tile, tile), tile)
+            product = jnp.dot(
+                a_buf[at, part, pl.ds(column, size)],
+                b_buf[pl.ds(pl.multiple_of(begin, 128), size), :],
+                preferred_element_type=jnp.float32)
+
+            @pl.when(dist == 0)
+            def _():
+                total[part, :] = product
+
+            @pl.when(dist > 0)
+            def _():
+                total[part, :] += product
+
+    def at_distance(dist, part="all"):
+        if cut == 0:
+            if part == "own":
+                return
+            part = "all"
+        lax.fori_loop(0, 2, lambda j, c: (multiply(j, dist, part), c)[1], 0)
 
     def relay(d, carry):
-        for q in range(CHUNKS + lanes - 1):
+        for step, (o, q) in enumerate([(0, q) for q in range(CHUNKS)] + crossed):
             for k in range(2):
                 from_z = z - d if k == 0 else z + d
 
                 @pl.when((from_z >= 0) & (from_z < line))
                 def _():
-                    lane = w if q < CHUNKS else side(q - CHUNKS + 1)
-                    block = from_z * lanes + lane
-                    index = block * CHUNKS + min(q, last)
+                    block = from_z * lanes + side(o)
+                    index = block * CHUNKS + q
                     arrived(index)
-                    along(k, chunk(index), index, send_z.at[k, from_z] if q < CHUNKS else send_zb.at[k, block])
+                    along(k, chunk(index), index, send_zb.at[k, block] if o else send_z.at[k, from_z])
                     if q < last:
                         across(chunk(index), index, from_z)
 
-            if q == 2:
+            if step == CHUNKS // 3:
                 @pl.when(d == 2)
                 def _():
                     for source in far:
                         pltpu.make_async_copy(a_buf.at[source], a_buf.at[source], a_recv.at[source]).wait()
                         a_copy(a_buf.at[source], source, a_send_p.at[source], partner).start()
 
-            if q == 1:
+            if step == CHUNKS // 6:
                 @pl.when(d == line - 1)
                 def _():
                     at_distance(line - 3)
 
-            if q == last:
+            for when, dist, part in ((CHUNKS // 2, line - 2, "own"), (CHUNKS - 2, line - 2, "others"),
+                                     (CHUNKS - 1, line - 1, "own")):
+                if step == when:
+                    @pl.when(d == line - 1)
+                    def _():
+                        at_distance(dist, part)
+
+            if step == CHUNKS - 1:
                 @pl.when(d == 2)
                 def _():
                     for copy in mine:
@@ -160,13 +190,13 @@
                         source = x * 2 + 1 - bc
                         pltpu.make_async_copy(a_buf.at[source], a_buf.at[source], a_recv.at[source]).wait()
 
-                @pl.when(d >= 2)
-                def _():
-                    at_distance(d - 2 + d // (line - 1))
+                @pl.when((d >= 2) & (d < line - 1))
+                def _():
+                    at_distance(d - 2)
         return carry
 
     lax.fori_loop(1, line, relay, 0)
-    at_distance(line - 1)
+    at_distance(line - 1, "others")
 
     def squares(t, c):
         v = total[pl.ds(pl.multiple_of(t * tile, tile), tile), :]
@@ -189,13 +219,6 @@
         everything = everything + stats[g]
     rms = jnp.sqrt(everything / (rows * n_ga) + 1e-06)
     rms_out[...] = rms
-    scale = 1.0 / rms
-
-    @pl.loop(0, rows // tile)
-    def _(t):
-        part = pl.ds(pl.multiple_of(t * tile, tile), tile)
-        out[part, :] = (total[part, :] * scale).astype(jnp.bfloat16)
-
     for o in range(1, n_ga):
         share(o, lax.rem(me + o, n_ga), me).wait_send()
     for o, target in enumerate(far):
@@ -213,7 +236,7 @@
             def _():
                 sent(CHUNKS, send_z.at[k, from_z])
                 for o in range(1, lanes):
-                    sent(1, send_zb.at[k, from_z * lanes + side(o)])
+                    sent(CROSS, send_zb.at[k, from_z * lanes + side(o)])
         for o in range(1, lanes):
             @pl.when(z == from_z)
             def _():
@@ -233,16 +256,15 @@
         rows, width = coef.shape
         depth, columns = rot.shape
         dma = pltpu.SemaphoreType.DMA
-        out, rms = pl.pallas_call(
+        rotated, rms = pl.pallas_call(
             functools.partial(kernel, n_ga, n_ba, line),
-            out_shape=(jax.ShapeDtypeStruct((rows, columns), jnp.bfloat16),
-                       jax.ShapeDtypeStruct((1, columns), jnp.float32)),
-            in_specs=[pl.BlockSpec(memory_space=pl.ANY)] * 2,
+            out_shape=(pltpu.VMEM((rows, columns), jnp.float32),
+                       pltpu.VMEM((1, columns), jnp.float32)),
+            in_specs=[pl.BlockSpec(memory_space=pltpu.HBM)] * 2,
             out_specs=(pl.BlockSpec(memory_space=pltpu.VMEM),) * 2,
             scratch_shapes=[
                 pltpu.VMEM((n_ba, rows, width), jnp.bfloat16),
                 pltpu.VMEM((n_ga * depth, columns), jnp.bfloat16),
-                pltpu.VMEM((rows, columns), jnp.float32),
                 pltpu.VMEM((n_ga, 1, columns), jnp.float32),
                 dma((n_ga * CHUNKS,)),
                 dma((2, line)),
@@ -256,9 +278,9 @@
                 dma((2,)),
             ],
             compiler_params=pltpu.CompilerParams(
-                collective_id=0, has_side_effects=True, vmem_limit_bytes=67043328),
-        )(coef, rot)
-        return out, rms.reshape(columns)
+                collective_id=0, has_side_effects=True, vmem_limit_bytes=48 * 2**20),
+        )(*(pltpu.with_memory_space_constraint(x, pltpu.HBM) for x in (coef, rot)))
+        return (rotated * (1.0 / rms)).astype(jnp.bfloat16), rms.reshape(columns)
 
     return jax.shard_map(body, mesh=mesh, in_specs=(P("ga", "ba"), P("ga", "ba")),
                          out_specs=(P("ga", "ba"), P("ba")), check_vma=False)

time: 206 us -> 199 us (0.966)
  Pallas kernels: 199 us -> 194 us
  local copies, waits for them, and re-layouts: 4.29 us -> 0 us
  other arithmetic: 1.31 us -> 3.56 us
    pallas_call x1, Pallas kernels: 199 us -> 194 us  [body(): pl.pallas_call(functools.partial(kernel, n_ga, n_ba, line), out_shape=(pl...]
    unnamed x1 -> x0, local copies, waits for them, and re-layouts: 4.29 us -> none
    convert_element_type x0 -> x1, other arithmetic: none -> 2.93 us  [body(): return ((rotated * (1.0 / rms)).astype(jnp.bfloat16), rms.reshape(columns))]
where the time goes in v2:
time: 199 us; the launch traced here: 198 us
  Pallas kernels  194 us (97%)
  other arithmetic  3.56 us (2%)
    pallas_call x1, Pallas kernels, body(): pl.pallas_call(functools.partial(kernel, n_ga, n_ba, line), out_shape=(pl...  194 us

profile of v2, /device:TPU:0, one launch (start us, length us, event | category | flops | bytes accessed | tf_op | source)
XLA Modules:
  0.0 198.4 jit_solution(10256318491730015692)
XLA Ops:
  0.6 194.2 %shard_map.41 = (f32[1280,1536]{1,0:T(8,128)S(1)}, f32[1,1536]{1,0:T(1,128)S(1)}) custom-call(bf16[1280,1536]{1,0:T(8,128)(2,1)} %coef.1, bf16[768,1536]{1,0:T(8,128)(2,1)} %rot.1), custom_call_target="tpu_custom_call" | custom-call | tf_op jit(solution)/shard_map/pallas_call | solution.py:259
  194.9 0.6 fusion
  195.5 2.9 %multiply_convert_fusion = bf16[1280,1536]{1,0:T(8,128)(2,1)} fusion(f32[1280,1536]{1,0:T(8,128)S(1)} %get-tuple-element.4, f32[1536]{0:T(1024)S(1)} %get-tuple-element.7), kind=kLoop, calls=%fused_computation | loop fusion | flops 3932160 | bytes 11802624 | tf_op jit(solution)/shard_map/convert_element_type | solution.py:283

commit v3 on v2

--- a/solution.py
+++ b/solution.py
@@ -34,11 +34,25 @@
     def chunk(index):
         return b_buf.at[pl.ds(pl.multiple_of(index * piece, piece), piece)]
 
+    partner = mb + 1 - 2 * bc
+    far = [lax.rem(bx + o, half) * 2 + bc for o in range(1, half)]
+
     barrier = pltpu.get_barrier_semaphore()
-    for o in range(1, n_ga):
-        pl.semaphore_signal(barrier, inc=1, device_id=ga(lax.rem(me + o, n_ga)), device_id_type=MESH)
-    for o in range(1, n_ba):
-        pl.semaphore_signal(barrier, inc=1, device_id={"ba": lax.rem(mb + o, n_ba)}, device_id_type=MESH)
+    def greet(device):
+        pl.semaphore_signal(barrier, inc=1, device_id=device, device_id_type=MESH)
+
+    @pl.when(z > 0)
+    def _():
+        greet(ga(me - lanes))
+
+    @pl.when(z < line - 1)
+    def _():
+        greet(ga(me + lanes))
+
+    for o in range(1, lanes):
+        greet(ga(z * lanes + side(o)))
+    for target in [*far, partner]:
+        greet({"ba": target})
 
     mine = [
         pltpu.make_async_copy(rot, b_buf.at[pl.ds(pl.multiple_of(me * depth, depth), depth)], own.at[0]),
@@ -46,7 +60,8 @@
     ]
     for copy in mine:
         copy.start()
-    pl.semaphore_wait(barrier, n_ga - 1 + n_ba - 1)
+    ends = (line - 1 - z) // (line - 1) + z // (line - 1)
+    pl.semaphore_wait(barrier, 2 - ends + lanes - 1 + len(far) + 1)
 
     def remote(src, index, sem, target):
         return pltpu.make_async_remote_copy(
@@ -83,8 +98,6 @@
             src_ref=src, dst_ref=a_buf.at[index], send_sem=sem, recv_sem=a_recv.at[index],
             device_id={"ba": target}, device_id_type=MESH)
 
-    partner = mb + 1 - 2 * bc
-    far = [lax.rem(bx + o, half) * 2 + bc for o in range(1, half)]
     for o, target in enumerate(far):
         a_copy(coef, mb, a_send_x.at[o], target).start()
     a_copy(coef, mb, a_send_p.at[mb], partner).start()
@@ -113,12 +126,12 @@
                 return
             for o in range(1, lanes):
                 block = from_z * lanes + side(o)
-                for q in range(cut):
+                for q in range(cut) if part == "cut" else range(cut, last):
                     arrived(block * CHUNKS + q)
-                panel(block * depth, cut * piece, dist)
-                for q in range(cut, last):
-                    arrived(block * CHUNKS + q)
-                panel(block * depth + cut * piece, depth - cut * piece, dist)
+                if part == "cut":
+                    panel(block * depth, cut * piece, dist)
+                else:
+                    panel(block * depth + cut * piece, depth - cut * piece, dist)
 
     cut = max(q for q in range(last) if q * piece % 128 == 0) if depth % 128 == 0 else 0
 
@@ -143,7 +156,7 @@
 
     def at_distance(dist, part="all"):
         if cut == 0:
-            if part == "own":
+            if part in ("own", "cut"):
                 return
             part = "all"
         lax.fori_loop(0, 2, lambda j, c: (multiply(j, dist, part), c)[1], 0)
@@ -174,8 +187,9 @@
                 def _():
                     at_distance(line - 3)
 
-            for when, dist, part in ((CHUNKS // 2, line - 2, "own"), (CHUNKS - 2, line - 2, "others"),
-                                     (CHUNKS - 1, line - 1, "own")):
+            for when, dist, part in ((CHUNKS // 2, line - 2, "own"), (CHUNKS - 2, line - 2, "cut"),
+                                     (CHUNKS - 2, line - 2, "rest"), (CHUNKS - 1, line - 1, "own"),
+                                     (CHUNKS - 1, line - 1, "cut")):
                 if step == when:
                     @pl.when(d == line - 1)
                     def _():
@@ -196,7 +210,7 @@
         return carry
 
     lax.fori_loop(1, line, relay, 0)
-    at_distance(line - 1, "others")
+    at_distance(line - 1, "rest")
 
     def squares(t, c):
         v = total[pl.ds(pl.multiple_of(t * tile, tile), tile), :]

time: 199 us -> 195 us (0.980)
  Pallas kernels: 194 us -> 191 us
    pallas_call x1, Pallas kernels: 194 us -> 191 us  [body(): pl.pallas_call(functools.partial(kernel, n_ga, n_ba, line), out_shape=(pl...]
where the time goes in v3:
time: 195 us
  Pallas kernels  191 us (98%)
  other arithmetic  3.56 us (2%)
    pallas_call x1, Pallas kernels, body(): pl.pallas_call(functools.partial(kernel, n_ga, n_ba, line), out_shape=(pl...  191 us

profile of v3, /device:TPU:0, one launch (start us, length us, event | category | flops | bytes accessed | tf_op | source)
XLA Modules:
  0.0 195.1 jit_solution(8444225815129409831)
XLA Ops:
  0.6 190.9 %shard_map.41 = (f32[1280,1536]{1,0:T(8,128)S(1)}, f32[1,1536]{1,0:T(1,128)S(1)}) custom-call(bf16[1280,1536]{1,0:T(8,128)(2,1)} %coef.1, bf16[768,1536]{1,0:T(8,128)(2,1)} %rot.1), custom_call_target="tpu_custom_call" | custom-call | tf_op jit(solution)/shard_map/pallas_call | solution.py:273
  191.5 0.6 fusion
  192.1 2.9 %multiply_convert_fusion = bf16[1280,1536]{1,0:T(8,128)(2,1)} fusion(f32[1280,1536]{1,0:T(8,128)S(1)} %get-tuple-element.4, f32[1536]{0:T(1024)S(1)} %get-tuple-element.7), kind=kLoop, calls=%fused_computation | loop fusion | flops 3932160 | bytes 11802624 | tf_op jit(solution)/shard_map/convert_element_type | solution.py:297

commit v4 on v3

--- a/solution.py
+++ b/solution.py
@@ -58,8 +58,6 @@
         pltpu.make_async_copy(rot, b_buf.at[pl.ds(pl.multiple_of(me * depth, depth), depth)], own.at[0]),
         pltpu.make_async_copy(coef, a_buf.at[mb], own.at[1]),
     ]
-    for copy in mine:
-        copy.start()
     ends = (line - 1 - z) // (line - 1) + z // (line - 1)
     pl.semaphore_wait(barrier, 2 - ends + lanes - 1 + len(far) + 1)
 
@@ -101,6 +99,8 @@
     for o, target in enumerate(far):
         a_copy(coef, mb, a_send_x.at[o], target).start()
     a_copy(coef, mb, a_send_p.at[mb], partner).start()
+    for copy in mine:
+        copy.start()
 
     for o, q in crossed:
         index = (z * lanes + side(o)) * CHUNKS + q
@@ -108,7 +108,7 @@
         for k in range(2):
             along(k, chunk(index), index, send_zb.at[k, z * lanes + side(o)])
 
-    tile = math.gcd(rows, 256)
+    tile = math.gcd(rows, 1280)
 
     def multiply(j, dist, part):
         from_z = z - dist + 2 * dist * j

time: 195 us -> 194 us (level)
  no operation moved by 1% of the time
where the time goes in v4:
time: 194 us
  Pallas kernels  190 us (98%)
  other arithmetic  3.56 us (2%)
    pallas_call x1, Pallas kernels, body(): pl.pallas_call(functools.partial(kernel, n_ga, n_ba, line), out_shape=(pl...  190 us

profile of v4, /device:TPU:0, one launch (start us, length us, event | category | flops | bytes accessed | tf_op | source)
XLA Modules:
  0.0 194.3 jit_solution(10132732712249216167)
XLA Ops:
  0.6 190.1 %shard_map.41 = (f32[1280,1536]{1,0:T(8,128)S(1)}, f32[1,1536]{1,0:T(1,128)S(1)}) custom-call(bf16[1280,1536]{1,0:T(8,128)(2,1)} %coef.1, bf16[768,1536]{1,0:T(8,128)(2,1)} %rot.1), custom_call_target="tpu_custom_call" | custom-call | tf_op jit(solution)/shard_map/pallas_call | solution.py:273
  190.8 0.6 fusion
  191.4 2.9 %multiply_convert_fusion = bf16[1280,1536]{1,0:T(8,128)(2,1)} fusion(f32[1280,1536]{1,0:T(8,128)S(1)} %get-tuple-element.4, f32[1536]{0:T(1024)S(1)} %get-tuple-element.7), kind=kLoop, calls=%fused_computation | loop fusion | flops 3932160 | bytes 11802624 | tf_op jit(solution)/shard_map/convert_element_type | solution.py:297
